TPU v7x, 256 devices: a whole 4x4x8 slice. The times are simulated.
256 devices in a mesh: gx: 16 (over z, x_lo), gy: 16 (over y, x_hi, core).
Axes of the slice: x: 4 (x_hi: 2, x_lo: 2; x = x_hi * 2 + x_lo), y: 4, z: 8, core: 2. Of those that a mesh axis runs over, the one named last changes fastest.
Arguments:
- gradient: float32 [2048, 512], P('gx', 'gy'), may hold values from -6 to 6
- stat_old: float32 [2048, 2048], P('gx', 'gy'), may hold values from -1.001 to 1.001, as said below
Outputs:
- statistic: float32 [2048, 2048], P('gx', 'gy')
- inverse_root: float32 [2048, 2048], P('gx', 'gy')
Inputs may be any that keep to these rules, and one draw needn't show every extreme that they name: stat_old is symmetric positive semidefinite with unit diagonal, the Gram matrix of 2048 unit-length rows of 512 entries.
All inputs are finite; a program needn't handle non-finite values.
Results may differ from a plain program's by a relative error of at most 0.0003.
Values sent between devices are 32-bit elements.
A program may use at most 64 MiB of HBM per device.

v0:
```python
import jax
import jax.numpy as jnp
from jax import lax
from jax.sharding import Mesh
from jax.sharding import PartitionSpec as P

GY = ("gy_0", "gy_1", "gy_2")
GX = ("gx_0", "gx_1")
GX_GY = ("gx_0", "gx_1", "gy_0", "gy_1", "gy_2")


def gather_axes(array, axes, dim):
    filled = array
    for number in range(len(axes) - 1, -1, -1):
        filled = lax.all_gather(filled, axes[number], axis=dim, tiled=True)
    return filled


def folded(array, axes, dim, take_in, carry):
    everything = jax.tree.map(lambda part: gather_axes(part, axes, dim), array)
    return take_in(carry, everything, jnp.int32(0))


def spread(array, axes, root):
    array = jnp.where(lax.axis_index(axes) == root, array, jnp.zeros_like(array))
    for axis in axes:
        array = lax.psum(array, axis)
    return array


def over_axes(array, axes):
    for axis in axes:
        array = lax.psum(array, axis)
    return array


def matmul(leading, trailing):
    return jnp.dot(
        leading, trailing, preferred_element_type=jnp.float32, precision=lax.Precision.HIGHEST
    )


def panels(factor_one, factor_two):
    whole_row = lax.all_gather(factor_one, GY, axis=1, tiled=True)

    def accumulate(running, shard_rows, first_row):
        matching = lax.dynamic_slice_in_dim(whole_row, first_row, shard_rows.shape[0], 1)
        return running + matmul(matching, shard_rows)

    empty = jnp.zeros((factor_one.shape[0], factor_two.shape[1]), jnp.float32)
    return folded(factor_two, GX, 0, accumulate, empty)


def product(factor_one, factor_two):
    return panels(factor_one, factor_two)


def local(gradient, stat_old):
    count_rows = lax.axis_size(GX)
    count_cols = lax.axis_size(GY)
    factor = count_rows // count_cols
    piece_width = stat_old.shape[0]
    row_index = lax.axis_index(GX)
    col_index = lax.axis_index(GY)
    panel_rows = lax.all_gather(gradient, GY, axis=1, tiled=True)
    outer_parts = []
    for member in range(factor):
        column_rows = spread(panel_rows, GX, col_index * factor + member)
        outer_parts.append(matmul(panel_rows, column_rows.T))
    outer = jnp.concatenate(outer_parts, axis=1) / panel_rows.shape[1]
    statistic = 0.9 * stat_old + outer
    squares = over_axes(jnp.sum(statistic * statistic), GX_GY)
    divisor = 2.0 * jnp.sqrt(squares / (piece_width * count_rows))
    global_rows = row_index * piece_width + lax.broadcasted_iota(jnp.int32, stat_old.shape, 0)
    global_cols = col_index * (factor * piece_width) + lax.broadcasted_iota(
        jnp.int32, stat_old.shape, 1
    )
    identity = (global_rows == global_cols).astype(jnp.float32)
    normed = statistic / divisor
    first_step = 1.5 * identity - 0.5 * normed
    root_half = product(normed, first_step)
    product_mid = product(first_step, root_half)
    second_step = 1.5 * identity - 0.5 * product_mid
    inverse_root = product(second_step, first_step)
    return (statistic, inverse_root)


def solution(mesh):
    torus = Mesh(mesh.devices.reshape(8, 2, 4, 2, 2), ("gx_0", "gx_1", "gy_0", "gy_1", "gy_2"))
    placed = (P(GX, GY), P(GX, GY))
    return jax.shard_map(
        local, mesh=torus, in_specs=placed, out_specs=(P(GX, GY), P(GX, GY)), check_vma=False
    )
```

profile of v0, /device:TPU:1, one launch (start us, length us, event | category | flops | bytes accessed | tf_op | source)
XLA Modules:
  0.0 435.5 jit_solution(8363940582427046131)
XLA Ops:
  7.2 0.0 copy-start.3
  7.2 0.0 all-reduce.3.cloned.1.call-start
  7.2 0.7 copy-done.3
  7.9 26.8 %all_gather.26 = f32[128,512]{0,1:T(8,128)S(1)} all-gather(f32[128,32]{0,1:T(8,128)S(1)} %copy-done.3), channel_id=1, replica_groups=mesh['gx_0'=8,'gx_1'=2,'gy_0'=4,'gy_1'=2,'gy_2'=2] {'gy_0','gy_1','gy_2'}, dimensions={1}, use_global_device_ids=true | all-gather | bytes 278528 | tf_op jit(solution)/shard_map/all_gather | solution.py:65
  34.6 0.7 broadcast_select_fusion
  35.4 0.0 all-reduce.3.cloned.1.call-update
  35.4 0.0 all-reduce.5.cloned.1.call-start
  35.4 65.4 %all-reduce.3.cloned.1.call-done = f32[128,512]{0,1:T(8,128)} async-done(((f32[128,512]{0,1:T(8,128)}), f32[128,512]{0,1:T(8,128)}) %all-reduce.3.cloned.1.call-update) | async-done | bytes 262160 | tf_op jit(solution)/shard_map/psum | solution.py:27
  100.8 0.0 copy-start.2
  100.8 0.0 all-reduce.5.cloned.1.call-update
  100.8 0.0 all-gather.10.cloned.1.call-start
  100.9 0.8 copy-done.2
  101.6 0.1 copy.4
  101.7 39.7 %all-reduce.5.cloned.1.call-done = f32[128,512]{0,1:T(8,128)} async-done(((f32[128,512]{0,1:T(8,128)}), f32[128,512]{0,1:T(8,128)}) %all-reduce.5.cloned.1.call-update) | async-done | bytes 262160 | tf_op jit(solution)/shard_map/psum | solution.py:27
  141.4 2.1 multiply_reduce_fusion
  143.6 14.6 %psum.51 = f32[]{:T(128)} all-reduce(f32[]{:T(128)} %get-tuple-element.6), channel_id=1, replica_groups=mesh['gx_0'=8,'gx_1'=2,'gy_0'=4,'gy_1'=2,'gy_2'=2] {'gx_0'}, use_global_device_ids=true, to_apply=%region_3.4 | all-reduce | flops 1 | bytes 8 | tf_op jit(solution)/shard_map/psum | solution.py:33
  158.1 4.4 %psum.52 = f32[]{:T(128)} all-reduce(f32[]{:T(128)} %psum.51), channel_id=1, replica_groups=mesh['gx_0'=8,'gx_1'=2,'gy_0'=4,'gy_1'=2,'gy_2'=2] {'gx_1'}, use_global_device_ids=true, to_apply=%region_4.5 | all-reduce | flops 1 | bytes 8 | tf_op jit(solution)/shard_map/psum | solution.py:33
  162.5 9.1 %psum.53 = f32[]{:T(128)} all-reduce(f32[]{:T(128)} %psum.52), channel_id=1, replica_groups=mesh['gx_0'=8,'gx_1'=2,'gy_0'=4,'gy_1'=2,'gy_2'=2] {'gy_0'}, use_global_device_ids=true, to_apply=%region_5.6 | all-reduce | flops 1 | bytes 8 | tf_op jit(solution)/shard_map/psum | solution.py:33
  171.6 5.9 %psum.54 = f32[]{:T(128)} all-reduce(f32[]{:T(128)} %psum.53), channel_id=1, replica_groups=mesh['gx_0'=8,'gx_1'=2,'gy_0'=4,'gy_1'=2,'gy_2'=2] {'gy_1'}, use_global_device_ids=true, to_apply=%region_6.7 | all-reduce | flops 1 | bytes 8 | tf_op jit(solution)/shard_map/psum | solution.py:33
  177.5 11.8 %psum.55 = f32[]{:T(128)} all-reduce(f32[]{:T(128)} %psum.54), channel_id=1, replica_groups=mesh['gx_0'=8,'gx_1'=2,'gy_0'=4,'gy_1'=2,'gy_2'=2] {'gy_2'}, use_global_device_ids=true, to_apply=%region_7.8 | all-reduce | flops 1 | bytes 8 | tf_op jit(solution)/shard_map/psum | solution.py:33
  190.0 0.6 select_subtract_fusion
  190.6 0.0 copy-start.1
  190.6 3.9 all_gather.29
  194.5 0.0 copy-done.1
  194.5 0.0 all-gather.10.cloned.1.call-update
  194.5 0.0 all-gather.8.cloned.1.call-start
  194.6 0.5 all-gather.8.cloned.1.call-update
  195.1 0.0 all-gather.6.cloned.1.call-start
  195.1 0.5 all-gather.6.cloned.1.call-update
  195.7 0.0 all-gather.12.cloned.1.call-start
  195.7 29.4 %all-gather.10.cloned.1.call-done = f32[2048,128]{0,1:T(8,128)} async-done(((f32[256,128]{0,1:T(8,128)}), f32[2048,128]{0,1:T(8,128)}) %all-gather.10.cloned.1.call-update) | async-done | bytes 1048592 | tf_op jit(solution)/shard_map/all_gather | solution.py:15
  225.1 56.8 %all-gather.8.cloned.1.call-done = f32[128,2048]{0,1:T(8,128)} async-done(((f32[128,128]{0,1:T(8,128)}), f32[128,2048]{0,1:T(8,128)}) %all-gather.8.cloned.1.call-update) | async-done | bytes 1048592 | tf_op jit(solution)/shard_map/all_gather | solution.py:44
  281.9 3.4 fusion.3
  285.2 3.9 all_gather.31
  289.1 0.0 all-gather.12.cloned.1.call-update
  289.1 0.0 copy-start
  289.1 0.0 all-gather.14.cloned.1.call-start
  289.2 44.5 %all-gather.6.cloned.1.call-done = f32[128,2048]{0,1:T(8,128)} async-done(((f32[128,128]{0,1:T(8,128)}), f32[128,2048]{0,1:T(8,128)}) %all-gather.6.cloned.1.call-update) | async-done | bytes 1048592 | tf_op jit(solution)/shard_map/all_gather | solution.py:44
  333.7 33.6 %all-gather.12.cloned.1.call-done = f32[2048,128]{1,0:T(8,128)} async-done(((f32[256,128]{1,0:T(8,128)}), f32[2048,128]{1,0:T(8,128)}) %all-gather.12.cloned.1.call-update) | async-done | bytes 1048592 | tf_op jit(solution)/shard_map/all_gather | solution.py:15
  367.3 4.0 fusion
  371.3 0.0 all-gather.14.cloned.1.call-update
  371.3 0.7 copy.5
  372.0 53.0 %all-gather.14.cloned.1.call-done = f32[128,2048]{0,1:T(8,128)} async-done(((f32[128,128]{0,1:T(8,128)}), f32[128,2048]{0,1:T(8,128)}) %all-gather.14.cloned.1.call-update) | async-done | bytes 1048592 | tf_op jit(solution)/shard_map/all_gather | solution.py:44
  425.0 0.0 copy-done
  425.0 3.7 fusion.4
  (1 shorter events, 0.0 us)
Async XLA Ops:
  7.2 0.7 copy-start.3
  7.2 93.6 %all-reduce.3.cloned.1.call-start = ((), (), s32[]{:S(2)}) async-start(), calls=%async_computation | async-start | bytes 524288 | tf_op jit(solution)/shard_map/psum | solution.py:27
  35.4 106.1 %all-reduce.5.cloned.1.call-start = ((), (), s32[]{:S(2)}) async-start(), calls=%async_computation.1 | async-start | bytes 524288 | tf_op jit(solution)/shard_map/psum | solution.py:27
  100.8 0.8 copy-start.2
  100.8 124.2 %all-gather.10.cloned.1.call-start = ((), (), s32[]{:S(2)}) async-start(), calls=%async_computation.4 | async-start | bytes 1179648 | tf_op jit(solution)/shard_map/all_gather | solution.py:15
  190.6 3.9 copy-start.1
  194.5 87.3 %all-gather.8.cloned.1.call-start = ((), (), s32[]{:S(2)}) async-start(), calls=%async_computation.3 | async-start | bytes 1114112 | tf_op jit(solution)/shard_map/all_gather | solution.py:44
  195.1 138.6 %all-gather.6.cloned.1.call-start = ((), (), s32[]{:S(2)}) async-start(), calls=%async_computation.2 | async-start | bytes 1114112 | tf_op jit(solution)/shard_map/all_gather | solution.py:44
  195.7 171.6 %all-gather.12.cloned.1.call-start = ((), (), s32[]{:S(2)}) async-start(), calls=%async_computation.5 | async-start | bytes 1179648 | tf_op jit(solution)/shard_map/all_gather | solution.py:15
  289.1 135.9 %copy-start = (f32[2048,128]{0,1:T(8,128)S(1)}, f32[2048,128]{0,1:T(8,128)}, u32[]{:S(2)}) copy-start(f32[2048,128]{0,1:T(8,128)} %all-gather.10.cloned.1.call-done) | copy-start | bytes 3145732
  289.1 135.9 %all-gather.14.cloned.1.call-start = ((), (), s32[]{:S(2)}) async-start(), calls=%async_computation.6 | async-start | bytes 1114112 | tf_op jit(solution)/shard_map/all_gather | solution.py:44
Sparse Core Ops, SparseCore 0:
  35.5 65.2 all-reduce.2
  103.4 38.0 all-reduce.4
  194.6 30.4 all-gather.9
  228.3 53.5 all-gather.7
  285.0 48.6 all-gather.5
  335.4 31.8 all-gather.11
  371.4 53.5 all-gather.13
where the time goes:
time: 436 us
  waiting for transfers between devices  323 us (74%)
  blocking collectives  80.2 us (18%)
  between operations  14.9 us (3%)
  matrix products  13.2 us (3%)
    all_gather x3, waiting for transfers between devices, panels(): whole_row = lax.all_gather(factor_one, GY, axis=1, tiled=True)  154 us
    psum x2, waiting for transfers between devices, spread(): array = lax.psum(array, axis)  105 us
    all_gather x2, waiting for transfers between devices, gather_axes(): filled = lax.all_gather(filled, axes[number], axis=dim, tiled=True)  62.9 us
    psum x5, blocking collectives, over_axes(): array = lax.psum(array, axis)  45.7 us
    all_gather x1, blocking collectives, local(): panel_rows = lax.all_gather(gradient, GY, axis=1, tiled=True)  26.8 us
    dot_general x4, matrix products, matmul(): jnp.dot(leading, trailing, preferred_element_type=jnp.float32, precision=...  13.2 us
  transfers between devices with their start and end apart: 7, of which 7 were waited for; matrix products, arithmetic and copies ran while one was open for 1% of the time, Pallas kernels for 0%

commit v1 on v0

--- a/solution.py
+++ b/solution.py
@@ -62,7 +62,19 @@
     piece_width = stat_old.shape[0]
     row_index = lax.axis_index(GX)
     col_index = lax.axis_index(GY)
-    panel_rows = lax.all_gather(gradient, GY, axis=1, tiled=True)
+
+    def yards_pair(vec, net_axis):
+        return jnp.concatenate(
+            lax.all_to_all(
+                jnp.stack(lax.axis_size(net_axis) * [vec]),
+                axis_name=net_axis,
+                split_axis=0,
+                concat_axis=0,
+            ),
+            axis=1,
+        )
+
+    panel_rows = yards_pair(gradient, GY)
     outer_parts = []
     for member in range(factor):
         column_rows = spread(panel_rows, GX, col_index * factor + member)

time: 436 us -> 428 us (0.982)
  blocking collectives: 80.2 us -> 53.4 us
  waiting for transfers between devices: 323 us -> 333 us
  starting transfers between devices: 0.28 us -> 8.71 us
    all_gather x1 -> x0, blocking collectives: 26.8 us -> none  [local(): panel_rows = lax.all_gather(gradient, GY, axis=1, tiled=True)]
    all_to_all x0 -> x1, waiting for transfers between devices: none -> 8.64 us  [yards_pair(): lax.all_to_all(jnp.stack(lax.axis_size(net_axis) * [vec]), axis_name=net_...]
    all_to_all x0 -> x1, starting transfers between devices: none -> 8.44 us  [yards_pair(): lax.all_to_all(jnp.stack(lax.axis_size(net_axis) * [vec]), axis_name=net_...]
  transfers between devices with their start and end apart: 7 -> 8, of which waited for: 7 -> 8; matrix products, arithmetic and copies ran while one was open for 1% -> 1% of each run, Pallas kernels for 0% -> 0%
where the time goes in v1:
time: 428 us
  waiting for transfers between devices  333 us (78%)
  blocking collectives  53.4 us (12%)
  between operations  14.9 us (3%)
  matrix products  13.2 us (3%)
  starting transfers between devices  8.71 us (2%)
    all_gather x3, waiting for transfers between devices, panels(): whole_row = lax.all_gather(factor_one, GY, axis=1, tiled=True)  154 us
    psum x2, waiting for transfers between devices, spread(): array = lax.psum(array, axis)  106 us
    all_gather x2, waiting for transfers between devices, gather_axes(): filled = lax.all_gather(filled, axes[number], axis=dim, tiled=True)  62.9 us
    psum x5, blocking collectives, over_axes(): array = lax.psum(array, axis)  45.7 us
    dot_general x4, matrix products, matmul(): jnp.dot(leading, trailing, preferred_element_type=jnp.float32, precision=...  13.2 us
    all_to_all x1, waiting for transfers between devices, yards_pair(): lax.all_to_all(jnp.stack(lax.axis_size(net_axis) * [vec]), axis_name=net_...  8.64 us
  transfers between devices with their start and end apart: 8, of which 8 were waited for; matrix products, arithmetic and copies ran while one was open for 1% of the time, Pallas kernels for 0%

profile of v1, /device:TPU:1, one launch (start us, length us, event | category | flops | bytes accessed | tf_op | source)
XLA Modules:
  0.0 427.7 jit_solution(2491505813099372437)
XLA Ops:
  7.2 1.4 stack.2
  8.6 8.4 %all-to-all-start = ((f32[16,128,32]{1,2,0:T(8,128)}), f32[16,128,32]{1,2,0:T(8,128)S(1)}, u32[]{:S(2)}, u32[]{:S(2)}) async-start(f32[16,128,32]{1,2,0:T(8,128)} %stack.2), calls=%async_computation | async-start | bytes 524288 | tf_op jit(solution)/shard_map/all_to_all | solution.py:68
  17.0 0.0 all-reduce.3.cloned.1.call-start
  17.1 8.6 %all-to-all-done = f32[16,128,32]{1,2,0:T(8,128)S(1)} async-done(((f32[16,128,32]{1,2,0:T(8,128)}), f32[16,128,32]{1,2,0:T(8,128)S(1)}, u32[]{:S(2)}, u32[]{:S(2)}) %all-to-all-start) | async-done | bytes 262176 | tf_op jit(solution)/shard_map/all_to_all | solution.py:68
  25.7 0.7 broadcast_select_fusion
  26.5 0.0 all-reduce.3.cloned.1.call-update
  26.5 0.0 all-reduce.5.cloned.1.call-start
  26.5 66.4 %all-reduce.3.cloned.1.call-done = f32[128,512]{0,1:T(8,128)} async-done(((f32[128,512]{0,1:T(8,128)}), f32[128,512]{0,1:T(8,128)}) %all-reduce.3.cloned.1.call-update) | async-done | bytes 262160 | tf_op jit(solution)/shard_map/psum | solution.py:27
  92.9 0.0 copy-start.2
  93.0 0.0 all-reduce.5.cloned.1.call-update
  93.0 0.0 all-gather.10.cloned.1.call-start
  93.0 0.8 copy-done.2
  93.8 0.1 copy.7
  93.9 39.7 %all-reduce.5.cloned.1.call-done = f32[128,512]{0,1:T(8,128)} async-done(((f32[128,512]{0,1:T(8,128)}), f32[128,512]{0,1:T(8,128)}) %all-reduce.5.cloned.1.call-update) | async-done | bytes 262160 | tf_op jit(solution)/shard_map/psum | solution.py:27
  133.6 2.1 multiply_reduce_fusion
  135.7 14.6 %psum.51 = f32[]{:T(128)} all-reduce(f32[]{:T(128)} %get-tuple-element.8), channel_id=1, replica_groups=mesh['gx_0'=8,'gx_1'=2,'gy_0'=4,'gy_1'=2,'gy_2'=2] {'gx_0'}, use_global_device_ids=true, to_apply=%region_3.4 | all-reduce | flops 1 | bytes 8 | tf_op jit(solution)/shard_map/psum | solution.py:33
  150.3 4.4 %psum.52 = f32[]{:T(128)} all-reduce(f32[]{:T(128)} %psum.51), channel_id=1, replica_groups=mesh['gx_0'=8,'gx_1'=2,'gy_0'=4,'gy_1'=2,'gy_2'=2] {'gx_1'}, use_global_device_ids=true, to_apply=%region_4.5 | all-reduce | flops 1 | bytes 8 | tf_op jit(solution)/shard_map/psum | solution.py:33
  154.7 9.1 %psum.53 = f32[]{:T(128)} all-reduce(f32[]{:T(128)} %psum.52), channel_id=1, replica_groups=mesh['gx_0'=8,'gx_1'=2,'gy_0'=4,'gy_1'=2,'gy_2'=2] {'gy_0'}, use_global_device_ids=true, to_apply=%region_5.6 | all-reduce | flops 1 | bytes 8 | tf_op jit(solution)/shard_map/psum | solution.py:33
  163.7 5.9 %psum.54 = f32[]{:T(128)} all-reduce(f32[]{:T(128)} %psum.53), channel_id=1, replica_groups=mesh['gx_0'=8,'gx_1'=2,'gy_0'=4,'gy_1'=2,'gy_2'=2] {'gy_1'}, use_global_device_ids=true, to_apply=%region_6.7 | all-reduce | flops 1 | bytes 8 | tf_op jit(solution)/shard_map/psum | solution.py:33
  169.6 11.8 %psum.55 = f32[]{:T(128)} all-reduce(f32[]{:T(128)} %psum.54), channel_id=1, replica_groups=mesh['gx_0'=8,'gx_1'=2,'gy_0'=4,'gy_1'=2,'gy_2'=2] {'gy_2'}, use_global_device_ids=true, to_apply=%region_7.8 | all-reduce | flops 1 | bytes 8 | tf_op jit(solution)/shard_map/psum | solution.py:33
  182.1 0.6 select_subtract_fusion
  182.7 0.0 copy-start.1
  182.7 3.9 all_gather.25
  186.6 0.0 copy-done.1
  186.6 0.0 all-gather.10.cloned.1.call-update
  186.6 0.0 all-gather.8.cloned.1.call-start
  186.7 0.5 all-gather.8.cloned.1.call-update
  187.2 0.0 all-gather.6.cloned.1.call-start
  187.3 0.5 all-gather.6.cloned.1.call-update
  187.8 0.0 all-gather.12.cloned.1.call-start
  187.9 29.4 %all-gather.10.cloned.1.call-done = f32[2048,128]{0,1:T(8,128)} async-done(((f32[256,128]{0,1:T(8,128)}), f32[2048,128]{0,1:T(8,128)}) %all-gather.10.cloned.1.call-update) | async-done | bytes 1048592 | tf_op jit(solution)/shard_map/all_gather | solution.py:15
  217.2 56.8 %all-gather.8.cloned.1.call-done = f32[128,2048]{0,1:T(8,128)} async-done(((f32[128,128]{0,1:T(8,128)}), f32[128,2048]{0,1:T(8,128)}) %all-gather.8.cloned.1.call-update) | async-done | bytes 1048592 | tf_op jit(solution)/shard_map/all_gather | solution.py:44
  274.0 3.4 fusion.3
  277.4 3.9 all_gather.27
  281.2 0.0 all-gather.12.cloned.1.call-update
  281.3 0.0 copy-start
  281.3 0.0 all-gather.14.cloned.1.call-start
  281.3 44.5 %all-gather.6.cloned.1.call-done = f32[128,2048]{0,1:T(8,128)} async-done(((f32[128,128]{0,1:T(8,128)}), f32[128,2048]{0,1:T(8,128)}) %all-gather.6.cloned.1.call-update) | async-done | bytes 1048592 | tf_op jit(solution)/shard_map/all_gather | solution.py:44
  325.9 33.6 %all-gather.12.cloned.1.call-done = f32[2048,128]{1,0:T(8,128)} async-done(((f32[256,128]{1,0:T(8,128)}), f32[2048,128]{1,0:T(8,128)}) %all-gather.12.cloned.1.call-update) | async-done | bytes 1048592 | tf_op jit(solution)/shard_map/all_gather | solution.py:15
  359.4 4.0 fusion
  363.4 0.0 all-gather.14.cloned.1.call-update
  363.5 0.7 copy.8
  364.2 53.0 %all-gather.14.cloned.1.call-done = f32[128,2048]{0,1:T(8,128)} async-done(((f32[128,128]{0,1:T(8,128)}), f32[128,2048]{0,1:T(8,128)}) %all-gather.14.cloned.1.call-update) | async-done | bytes 1048592 | tf_op jit(solution)/shard_map/all_gather | solution.py:44
  417.2 0.0 copy-done
  417.2 3.7 fusion.4
  (1 shorter events, 0.0 us)
Async XLA Ops:
  8.6 17.1 %all-to-all-start = ((f32[16,128,32]{1,2,0:T(8,128)}), f32[16,128,32]{1,2,0:T(8,128)S(1)}, u32[]{:S(2)}, u32[]{:S(2)}) async-start(f32[16,128,32]{1,2,0:T(8,128)} %stack.2), calls=%async_computation | async-start | bytes 524288 | tf_op jit(solution)/shard_map/all_to_all | solution.py:68
  17.0 75.9 %all-reduce.3.cloned.1.call-start = ((), (), s32[]{:S(2)}) async-start(), calls=%async_computation.1 | async-start | bytes 524288 | tf_op jit(solution)/shard_map/psum | solution.py:27
  26.5 107.1 %all-reduce.5.cloned.1.call-start = ((), (), s32[]{:S(2)}) async-start(), calls=%async_computation.2 | async-start | bytes 524288 | tf_op jit(solution)/shard_map/psum | solution.py:27
  92.9 0.8 copy-start.2
  93.0 124.2 %all-gather.10.cloned.1.call-start = ((), (), s32[]{:S(2)}) async-start(), calls=%async_computation.5 | async-start | bytes 1179648 | tf_op jit(solution)/shard_map/all_gather | solution.py:15
  182.7 3.9 copy-start.1
  186.6 87.3 %all-gather.8.cloned.1.call-start = ((), (), s32[]{:S(2)}) async-start(), calls=%async_computation.4 | async-start | bytes 1114112 | tf_op jit(solution)/shard_map/all_gather | solution.py:44
  187.2 138.6 %all-gather.6.cloned.1.call-start = ((), (), s32[]{:S(2)}) async-start(), calls=%async_computation.3 | async-start | bytes 1114112 | tf_op jit(solution)/shard_map/all_gather | solution.py:44
  187.8 171.6 %all-gather.12.cloned.1.call-start = ((), (), s32[]{:S(2)}) async-start(), calls=%async_computation.6 | async-start | bytes 1179648 | tf_op jit(solution)/shard_map/all_gather | solution.py:15
  281.3 135.9 %copy-start = (f32[2048,128]{0,1:T(8,128)S(1)}, f32[2048,128]{0,1:T(8,128)}, u32[]{:S(2)}) copy-start(f32[2048,128]{0,1:T(8,128)} %all-gather.10.cloned.1.call-done) | copy-start | bytes 3145732
  281.3 135.9 %all-gather.14.cloned.1.call-start = ((), (), s32[]{:S(2)}) async-start(), calls=%async_computation.7 | async-start | bytes 1114112 | tf_op jit(solution)/shard_map/all_gather | solution.py:44
Sparse Core Ops, SparseCore 0:
  26.6 66.3 all-reduce.2
  95.5 38.0 all-reduce.4
  186.8 30.4 all-gather.9
  220.4 53.5 all-gather.7
  277.2 48.6 all-gather.5
  327.5 31.8 all-gather.11
  363.6 53.5 all-gather.13
